TPU v7x, 512 devices: a 8x2x16 block of a 8x8x16 slice. The times are simulated.
512 devices in a mesh: groups: 2 (over y), req: 16 (over z), head: 8 (over x), sub: 2 (over core).
Axes of the slice: x: 8, y: 2, z: 16, core: 2. Of those that a mesh axis runs over, the one named last changes fastest.
The devices are a block of a 8x8x16 slice.
Arguments:
- q_nope: bfloat16 [8192, 8192], P(('groups', 'req', 'sub'), 'head'), parts along dimension 0, may hold values from -12 to 12
- q_rope: bfloat16 [8192, 4096], P(('groups', 'req', 'sub'), 'head'), parts along dimension 0, may hold values from -16 to 16
- new_latent: bfloat16 [8192, 512], P(('groups', 'req', 'sub')), parts along dimension 0, may hold values from -6 to 6
- new_rope: bfloat16 [8192, 64], P(('groups', 'req', 'sub')), parts along dimension 0, may hold values from -8 to 8
- pool_latent: bfloat16 [512, 128, 512], P(('groups', 'req'), None, 'sub'), parts along dimension 0, may hold values from -6 to 6
- pool_rope: bfloat16 [512, 128, 64], P(('groups', 'req')), parts along dimension 0, may hold values from -6 to 6
- w_uk: bfloat16 [512, 8192], P(None, 'head'), may hold values from -0.25 to 0.25
- w_uv: bfloat16 [512, 8192], P(None, 'head'), may hold values from -0.25 to 0.25
- block_list: int32 [32, 6], P(('groups', 'req')), parts along dimension 0, may hold values from 0 to 255, as said below
- prefix_len: int32 [32], P(('groups', 'req')), parts along dimension 0, may hold values from 192 to 768, as said below
- block_slot: int32 [512], P('groups'), parts along dimension 0, may hold values from 0 to 255, as said below
Outputs:
- attended: bfloat16 [8192, 8192], P(('groups', 'req', 'sub'), 'head'), parts along dimension 0
There are 2 independent parts, one for each index of `groups`. A program takes and returns all parts, laid end to end along the dimension named above; an argument that names none is the same for every part. Nothing has to cross between parts.
Inputs may be any that keep to these rules, and one draw needn't show every extreme that they name: `block_list`: each row lists 6 different block ids; no row lists more than 2 blocks stored with one owner (storage positions o * 16 to o * 16 + 15), and in every draw some owner stores 2 blocks of every row. `prefix_len`: some row has the full 6 * 128 prefix tokens. `block_slot`: each storage position once.
All inputs are finite; a program needn't handle non-finite values.
Results may differ from a plain program's by a relative error of at most 0.0072.
Values may be sent and summed in bfloat16 or wider, within the bound.
A program may use at most 64 MiB of HBM per device.

v0:
```python
import math

import jax
import jax.numpy as jnp
from jax import lax
from jax.sharding import PartitionSpec as P

NOPE = 128
ROPE = 64
VDIM = 128
CAP = 2


def side_by_side(arrays, axis, split_dim, concat_dim, along):
    both = jnp.concatenate(arrays, axis=along)
    whole, at, gathered = (
        lax.all_to_all(both, axis, split_axis=split_dim, concat_axis=concat_dim, tiled=True),
        0,
        [],
    )
    for a in arrays:
        gathered.append(lax.slice_in_dim(whole, at, at + a.shape[along], axis=along))
        at += a.shape[along]
    return tuple(gathered)


def copy_for_each(shard, axis):
    devices = lax.axis_size(axis)
    return lax.all_to_all(
        jnp.broadcast_to(shard[None], (devices, *shard.shape)), axis, 0, 0, tiled=True
    )


def in_order(tiles, dim):
    tiles = jnp.moveaxis(tiles, 0, dim)
    dims = tiles.shape
    return tiles.reshape(*dims[:dim], dims[dim] * dims[dim + 1], *dims[dim + 2 :])


def gathered_copies(shard, axis, dim):
    tiles = copy_for_each(shard, axis)
    return in_order(tiles, dim)


def sent_together(arrays, axis, dim, along):
    both = jnp.concatenate(arrays, axis=along)
    whole, at, gathered = (gathered_copies(both, axis, dim), 0, [])
    for a in arrays:
        gathered.append(lax.slice_in_dim(whole, at, at + a.shape[along], axis=along))
        at += a.shape[along]
    return tuple(gathered)


def in_one_piece(arrays, axis, dim, along):
    ends, at = ([], 0)
    for a in arrays[:-1]:
        at += a.shape[along]
        ends.append(at)
    both = jnp.concatenate(arrays, axis=along)
    return tuple(jnp.split(lax.all_gather(both, axis, axis=dim, tiled=True), ends, axis=along))


def shards(
    q_nope,
    q_rope,
    new_latent,
    new_rope,
    pool_latent,
    pool_rope,
    w_uk,
    w_uv,
    block_list,
    prefix_len,
    block_slot,
):
    owners = lax.axis_size("req")
    pool_local = pool_latent.shape[0]
    block = pool_latent.shape[1]
    blocks = block_list.shape[1]
    wanted = block_list[0]
    pool_ids = jnp.arange(block_slot.shape[0], dtype=jnp.int32)
    physical = jnp.sum(
        jnp.where(wanted[:, None] == pool_ids[None, :], block_slot[None, :], 0), axis=1
    )
    owner = physical // pool_local
    local = physical % pool_local
    order = jnp.arange(blocks, dtype=jnp.int32)
    earlier = jnp.sum(
        ((owner[None, :] == owner[:, None]) & (order[None, :] < order[:, None])).astype(jnp.int32),
        axis=1,
    )
    slot = owner * CAP + earlier
    slot_ids = jnp.arange(owners * CAP, dtype=jnp.int32)
    request = jnp.sum(jnp.where(slot[:, None] == slot_ids[None, :], local[:, None], 0), axis=0)
    request = request.reshape(owners, CAP)
    asked = lax.all_to_all(request, "req", split_axis=0, concat_axis=0, tiled=True).reshape(-1)
    width = block // lax.axis_size("head")
    begin = lax.axis_index("head") * width
    lat_part = lax.dynamic_slice_in_dim(pool_latent, begin, width, 1)
    rope_part = lax.dynamic_slice_in_dim(pool_rope, begin, width, 1)
    sent_lat = jnp.take(lat_part, asked, axis=0).reshape(owners, CAP, width, -1)
    sent_rope = jnp.take(rope_part, asked, axis=0).reshape(owners, CAP, width, -1)
    got_lat, got_rope = side_by_side((sent_lat, sent_rope), "req", 0, 0, 3)
    pick_lat = jnp.take(got_lat.reshape(owners * CAP, width, -1), slot, axis=0)
    pick_rope = jnp.take(got_rope.reshape(owners * CAP, width, -1), slot, axis=0)
    prefix_lat, prefix_rope = sent_together((pick_lat, pick_rope), "head", 1, 2)
    prefix_lat = lax.all_gather(prefix_lat, "sub", axis=2, tiled=True)
    fresh_lat, fresh_rope = in_one_piece((new_latent, new_rope), "sub", 0, 1)
    prefix = blocks * block
    key_latent = jnp.concatenate([prefix_lat.reshape(prefix, -1), fresh_lat], axis=0)
    key_rope = jnp.concatenate([prefix_rope.reshape(prefix, -1), fresh_rope], axis=0)
    total = key_latent.shape[0]
    heads = w_uk.shape[1] // NOPE
    key_nope = (
        jnp.dot(key_latent, w_uk, preferred_element_type=jnp.float32)
        .astype(jnp.bfloat16)
        .reshape(total, heads, NOPE)
    )
    values = (
        jnp.dot(key_latent, w_uv, preferred_element_type=jnp.float32)
        .astype(jnp.bfloat16)
        .reshape(total, heads, VDIM)
    )
    queries_here = q_nope.shape[0]
    query_nope = q_nope.reshape(queries_here, heads, NOPE)
    query_rope = q_rope.reshape(queries_here, heads, ROPE)
    scores = jnp.einsum("qhd,khd->hqk", query_nope, key_nope, preferred_element_type=jnp.float32)
    scores = scores + jnp.einsum(
        "qhd,kd->hqk", query_rope, key_rope, preferred_element_type=jnp.float32
    )
    scores = scores * (1.0 / math.sqrt(NOPE + ROPE))
    key_pos = jnp.arange(total, dtype=jnp.int32)
    query_pos = lax.axis_index("sub") * queries_here + jnp.arange(queries_here, dtype=jnp.int32)
    visible = jnp.where(
        key_pos[None, :] < prefix,
        key_pos[None, :] < prefix_len[0],
        key_pos[None, :] - prefix <= query_pos[:, None],
    )
    scores = jnp.where(visible[None], scores, jnp.float32(-1e30))
    peak = jnp.max(scores, axis=2, keepdims=True)
    expo = jnp.where(visible[None], jnp.exp(scores - peak), jnp.float32(0.0))
    weights = (expo / jnp.sum(expo, axis=2, keepdims=True)).astype(jnp.bfloat16)
    out = jnp.einsum("hqk,khd->qhd", weights, values, preferred_element_type=jnp.float32)
    return out.astype(jnp.bfloat16).reshape(queries_here, heads * VDIM)


def solution(mesh):
    placed = (
        P(("groups", "req", "sub"), "head"),
        P(("groups", "req", "sub"), "head"),
        P(("groups", "req", "sub"), None),
        P(("groups", "req", "sub"), None),
        P(("groups", "req"), None, "sub"),
        P(("groups", "req"), None, None),
        P(None, "head"),
        P(None, "head"),
        P(("groups", "req"), None),
        P(("groups", "req")),
        P("groups"),
    )
    return jax.shard_map(
        shards,
        mesh=mesh,
        in_specs=placed,
        out_specs=P(("groups", "req", "sub"), "head"),
        check_vma=False,
    )
```

profile of v0, /device:TPU:65, one launch (start us, length us, event | category | flops | bytes accessed | tf_op | source)
XLA Modules:
  0.0 132.0 jit_solution(14055643360750967935)
XLA Ops:
  0.0 0.0 copy-start
  0.0 0.9 select_reduce_fusion
  1.0 0.2 convert_reduce_fusion
  1.2 0.1 select_reduce_fusion.1
  1.3 0.7 all_to_all.12
  1.9 44.2 %all-to-all-start = ((s32[16,1,2]{2,1,0:T(1,128)}), s32[16,1,2]{2,1,0:T(1,128)S(1)}, u32[]{:S(2)}, u32[]{:S(2)}) async-start(s32[16,1,2]{2,1,0:T(1,128)} %bitcast.1), calls=%async_computation | async-start | bytes 16384 | tf_op jit(solution)/shard_map/all_to_all | solution.py:96
  46.2 0.0 copy-start.3
  46.2 1.1 constant_dynamic-slice_fusion
  47.3 0.0 copy-start.5
  47.3 0.9 constant_dynamic-slice_fusion.1
  48.3 9.0 %all-to-all-done = s32[16,1,2]{2,1,0:T(1,128)S(1)} async-done(((s32[16,1,2]{2,1,0:T(1,128)}), s32[16,1,2]{2,1,0:T(1,128)S(1)}, u32[]{:S(2)}, u32[]{:S(2)}) %all-to-all-start) | async-done | bytes 160 | tf_op jit(solution)/shard_map/all_to_all | solution.py:96
  57.2 0.5 broadcast.353
  57.7 0.7 reduce.3
  58.4 0.1 reshape.273
  58.5 0.1 copy.50
  58.6 0.1 copy.51
  58.7 0.6 gather_fusion.1
  59.4 0.1 broadcast_select_fusion
  59.5 0.0 copy-start.4
  59.5 0.2 copy.53
  59.7 0.6 gather_fusion
  60.3 0.1 broadcast_select_fusion.1
  60.4 0.8 pad_maximum_fusion.3
  61.2 4.0 %all-to-all-start.1 = ((bf16[16,2,16,320]{3,2,1,0:T(8,128)(2,1)}), bf16[16,2,16,320]{3,2,1,0:T(8,128)(2,1)S(1)}, u32[]{:S(2)}, u32[]{:S(2)}) async-start(bf16[16,2,16,320]{3,2,1,0:T(8,128)(2,1)} %pad_maximum_fusion.3), calls=%async_computation.1 | async-start | bytes 786432 | tf_op jit(solution)/shard_map/all_to_all | solution.py:17
  65.2 17.7 %all-to-all-done.1 = bf16[16,2,16,320]{3,2,1,0:T(8,128)(2,1)S(1)} async-done(((bf16[16,2,16,320]{3,2,1,0:T(8,128)(2,1)}), bf16[16,2,16,320]{3,2,1,0:T(8,128)(2,1)S(1)}, u32[]{:S(2)}, u32[]{:S(2)}) %all-to-all-start.1) | async-done | bytes 327712 | tf_op jit(solution)/shard_map/all_to_all | solution.py:17
  83.0 0.6 gather_fusion.2
  83.6 0.6 gather_fusion.3
  84.1 0.1 broadcast_select_fusion.2
  84.2 0.1 broadcast_select_fusion.3
  84.3 0.9 broadcast_in_dim.133
  85.2 7.1 %all-to-all-start.2 = ((bf16[8,6,16,320]{3,2,1,0:T(8,128)(2,1)}), bf16[8,6,16,320]{3,2,1,0:T(8,128)(2,1)S(1)}, u32[]{:S(2)}, u32[]{:S(2)}) async-start(bf16[8,6,16,320]{3,2,1,0:T(8,128)(2,1)} %broadcast_in_dim.133), calls=%async_computation.2 | async-start | bytes 1179648 | tf_op jit(solution)/shard_map/all_to_all | solution.py:29
  92.2 0.0 copy-done.3
  92.2 0.1 copy.55
  92.4 0.0 copy-done.5
  92.4 8.1 %all_gather.7 = bf16[256,576]{0,1:T(8,128)(2,1)S(1)} all-gather(bf16[128,576]{0,1:T(8,128)(2,1)S(1)} %pad_maximum_fusion.4), channel_id=1, replica_groups=mesh['groups'=2,'req'=16,'head'=8,'sub'=2] {'sub'}, dimensions={0}, use_global_device_ids=true | all-gather | bytes 442368 | tf_op jit(solution)/shard_map/all_gather | solution.py:60
  100.5 0.0 copy-start.1
  100.5 0.1 copy.56
  101.3 0.0 copy-done.4
  101.3 0.1 copy.60
  101.5 0.9 compare_select_fusion
  102.4 2.9 %all-to-all-done.2 = bf16[8,6,16,320]{3,2,1,0:T(8,128)(2,1)S(1)} async-done(((bf16[8,6,16,320]{3,2,1,0:T(8,128)(2,1)}), bf16[8,6,16,320]{3,2,1,0:T(8,128)(2,1)S(1)}, u32[]{:S(2)}, u32[]{:S(2)}) %all-to-all-start.2) | async-done | bytes 491552 | tf_op jit(solution)/shard_map/all_to_all | solution.py:29
  105.2 0.1 copy.54
  105.4 9.4 %all_gather.6 = bf16[6,128,512]{2,1,0:T(8,128)(2,1)S(1)} all-gather(bf16[6,128,256]{2,1,0:T(8,128)(2,1)S(1)} %slice.26), channel_id=1, replica_groups=mesh['groups'=2,'req'=16,'head'=8,'sub'=2] {'sub'}, dimensions={2}, use_global_device_ids=true | all-gather | bytes 1179648 | tf_op jit(solution)/shard_map/all_gather | solution.py:107
  114.8 0.1 copy.65
  114.9 0.0 copy-start.6
  114.9 0.0 copy-done
  114.9 1.3 convolution_convert_fusion
  116.2 0.0 copy-done.1
  116.2 0.0 copy-done.6
  116.3 0.0 copy-start.2
  116.3 2.7 %convolution_convert_fusion.1 = bf16[1024,1024]{0,1:T(8,128)(2,1)} fusion(bf16[512,1024]{1,0:T(8,128)(2,1)S(1)} %copy-done.6, bf16[256,512]{1,0:T(8,128)(2,1)S(1)} %copy.56, bf16[768,512]{1,0:T(8,128)(2,1)S(1)} %bitcast.74), kind=kOutput, calls=%fused_computation.12 | convolution fusion | flops 1076887552 | bytes 4194304 | tf_op jit(solution)/shard_map/dot_general | solution.py:120
  119.0 0.0 slice-start
  119.0 0.0 copy-done.2
  119.0 2.8 %fusion.5 = f32[8,1024,128]{2,1,0:T(8,128)} fusion(bf16[1024,8,128]{0,2,1:T(8,128)(2,1)S(1)} %bitcast.70, bf16[128,1024]{1,0:T(8,128)(2,1)S(1)} %copy-done.2), kind=kOutput, calls=%fused_computation.18 | convolution fusion | flops 268435456 | bytes 6553600 | tf_op jit(solution)/shard_map/qhd,khd->hqk/dot_general | solution.py:127
  121.7 0.0 slice-done
  121.7 5.9 %fusion.16 = (f32[8,128]{1,0:T(8,128)S(1)}, f32[8,128,1024]{1,2,0:T(8,128)}) fusion(pred[128,1024]{0,1:T(8,128)(4,1)S(1)} %compare_select_fusion, f32[8,1024,128]{2,1,0:T(8,128)} %fusion.5, bf16[128,8,64]{0,2,1:T(8,128)(2,1)S(1)} %bitcast.79, bf16[256,64]{0,1:T(8,128)(2,1)S(1)} %slice-done, bf16[768,64]{0,1:T(8,128)(2,1)S(1)} %copy.65), kind=kOutput, calls=%fused_computation.67 | convolution fusion | flops 140772352 | bytes 8785920 | tf_op jit(solution)/shard_map/sub | solution.py:141
  127.6 3.5 %fusion.4 = bf16[8,128,128]{2,1,0:T(8,128)(2,1)S(1)} fusion(bf16[1024,8,128]{0,2,1:T(8,128)(2,1)} %bitcast.81, f32[8,128,1024]{1,2,0:T(8,128)} %get-tuple-element.10, f32[8,128]{1,0:T(8,128)S(1)} %get-tuple-element.9), kind=kOutput, calls=%fused_computation.13 | convolution fusion | flops 270663680 | bytes 6557696 | tf_op jit(solution)/shard_map/hqk,khd->qhd/dot_general | solution.py:143
  131.2 0.9 copy.62
  (17 shorter events, 0.2 us)
Async XLA Ops:
  0.0 114.9 %copy-start = (bf16[512,1024]{1,0:T(8,128)(2,1)S(1)}, bf16[512,1024]{1,0:T(8,128)(2,1)}, u32[]{:S(2)}) copy-start(bf16[512,1024]{1,0:T(8,128)(2,1)} %param.17) | copy-start | bytes 3145732
  1.9 55.3 %all-to-all-start = ((s32[16,1,2]{2,1,0:T(1,128)}), s32[16,1,2]{2,1,0:T(1,128)S(1)}, u32[]{:S(2)}, u32[]{:S(2)}) async-start(s32[16,1,2]{2,1,0:T(1,128)} %bitcast.1), calls=%async_computation | async-start | bytes 16384 | tf_op jit(solution)/shard_map/all_to_all | solution.py:96
  46.2 46.1 %copy-start.3 = (bf16[128,512]{1,0:T(8,128)(2,1)S(1)}, bf16[128,512]{1,0:T(8,128)(2,1)}, u32[]{:S(2)}) copy-start(bf16[128,512]{1,0:T(8,128)(2,1)} %param.13) | copy-start | bytes 393220
  47.3 45.0 %copy-start.5 = (bf16[128,64]{0,1:T(8,128)(2,1)S(1)}, bf16[128,64]{0,1:T(8,128)(2,1)}, u32[]{:S(2)}) copy-start(bf16[128,64]{0,1:T(8,128)(2,1)} %param.14) | copy-start | bytes 49156
  59.5 41.8 %copy-start.4 = (bf16[128,512]{1,0:T(8,128)(2,1)S(1)}, bf16[128,512]{1,0:T(8,128)(2,1)}, u32[]{:S(2)}) copy-start(bf16[128,512]{1,0:T(8,128)(2,1)} %param.12) | copy-start | bytes 393220
  61.2 21.8 %all-to-all-start.1 = ((bf16[16,2,16,320]{3,2,1,0:T(8,128)(2,1)}), bf16[16,2,16,320]{3,2,1,0:T(8,128)(2,1)S(1)}, u32[]{:S(2)}, u32[]{:S(2)}) async-start(bf16[16,2,16,320]{3,2,1,0:T(8,128)(2,1)} %pad_maximum_fusion.3), calls=%async_computation.1 | async-start | bytes 786432 | tf_op jit(solution)/shard_map/all_to_all | solution.py:17
  85.2 20.1 %all-to-all-start.2 = ((bf16[8,6,16,320]{3,2,1,0:T(8,128)(2,1)}), bf16[8,6,16,320]{3,2,1,0:T(8,128)(2,1)S(1)}, u32[]{:S(2)}, u32[]{:S(2)}) async-start(bf16[8,6,16,320]{3,2,1,0:T(8,128)(2,1)} %broadcast_in_dim.133), calls=%async_computation.2 | async-start | bytes 1179648 | tf_op jit(solution)/shard_map/all_to_all | solution.py:29
  100.5 15.8 %copy-start.1 = (bf16[256,576]{0,1:T(8,128)(2,1)}, bf16[256,576]{0,1:T(8,128)(2,1)S(1)}, u32[]{:S(2)}) copy-start(bf16[256,576]{0,1:T(8,128)(2,1)S(1)} %all_gather.7) | copy-start | bytes 884740
  114.9 1.3 %copy-start.6 = (bf16[512,1024]{1,0:T(8,128)(2,1)S(1)}, bf16[512,1024]{1,0:T(8,128)(2,1)}, u32[]{:S(2)}) copy-start(bf16[512,1024]{1,0:T(8,128)(2,1)} %param.18) | copy-start | bytes 3145732
  116.3 2.7 %copy-start.2 = (bf16[128,1024]{1,0:T(8,128)(2,1)S(1)}, bf16[128,1024]{1,0:T(8,128)(2,1)}, u32[]{:S(2)}) copy-start(bf16[128,1024]{1,0:T(8,128)(2,1)} %param.11) | copy-start | bytes 786436
  119.0 2.8 %slice-start = ((bf16[256,576]{0,1:T(8,128)(2,1)}), bf16[256,64]{0,1:T(8,128)(2,1)S(1)}, s32[]{:S(2)}) async-start(bf16[256,576]{0,1:T(8,128)(2,1)} %copy-done.1), calls=%async_computation.3 | async-start | bytes 65536 | tf_op jit(solution)/shard_map/split | solution.py:60
where the time goes:
time: 132 us
  starting transfers between devices  55.3 us (42%)
  waiting for transfers between devices  29.6 us (22%)
  blocking collectives  17.5 us (13%)
  matrix products  16.2 us (12%)
  local copies, waits for them, and re-layouts  8.51 us (6%)
  other arithmetic  4.02 us (3%)
    all_to_all x1, starting transfers between devices, shards(): lax.all_to_all(request, 'req', split_axis=0, concat_axis=0, tiled=True)  44.2 us
    all_to_all x1, waiting for transfers between devices, side_by_side(): lax.all_to_all(both, axis, split_axis=split_dim, concat_axis=concat_dim,...  17.7 us
    all_gather x1, blocking collectives, shards(): prefix_lat = lax.all_gather(prefix_lat, 'sub', axis=2, tiled=True)  9.4 us
    all_to_all x1, waiting for transfers between devices, shards(): lax.all_to_all(request, 'req', split_axis=0, concat_axis=0, tiled=True)  8.96 us
    all_gather x1, blocking collectives, in_one_piece(): lax.all_gather(both, axis, axis=dim, tiled=True)  8.08 us
    all_to_all x1, starting transfers between devices, copy_for_each(): lax.all_to_all(jnp.broadcast_to(shard[None], (devices, *shard.shape)), ax...  7.08 us
    sub x1, matrix products, shards(): expo = jnp.where(visible[None], jnp.exp(scores - peak), jnp.float32(0.0))  5.9 us
    all_to_all x1, starting transfers between devices, side_by_side(): lax.all_to_all(both, axis, split_axis=split_dim, concat_axis=concat_dim,...  3.99 us
  transfers between devices with their start and end apart: 3, of which 3 were waited for; matrix products, arithmetic and copies ran while one was open for 3% of the time, Pallas kernels for 0%

commit v1 on v0

v1 whole, which is shorter than its diff:
```python
import functools
import math

import jax
import jax.numpy as jnp
from jax import lax
from jax.experimental import pallas as pl
from jax.experimental.pallas import tpu as pltpu
from jax.sharding import PartitionSpec as P

NOPE = 128
ROPE = 64
VDIM = 128
CAP = 2
MESH = pl.DeviceIdType.MESH
BF = jnp.bfloat16
F32 = jnp.float32


def exchange(
    blocks,
    pool_local,
    list_ref,
    slot_ref,
    pool_lat,
    pool_rope,
    new_lat,
    new_rope,
    lat_mine,
    lat_other,
    rope_mine,
    rope_other,
    new_lat_other,
    new_rope_other,
    pool_l,
    pool_r,
    send_l,
    send_r,
    got_l,
    got_r,
    own_v,
    table_in,
    table_out,
    asked_v,
    table_s,
    asked_s,
    pool_sem,
    small_sem,
    hello_sem,
    table_sem,
    ask_send,
    ask_recv,
    lat_send,
    lat_recv,
    rope_send,
    rope_recv,
    xlat_send,
    xlat_recv,
    xrope_send,
    xrope_recv,
    slat_send,
    slat_recv,
    srope_send,
    srope_recv,
    snew_send,
    snew_recv,
):
    rows = lax.axis_size("req")
    heads = lax.axis_size("head")
    row = lax.axis_index("req")
    lane = lax.axis_index("head")
    core = lax.axis_index("sub")
    other = {"sub": 1 - core}
    carriers = heads // 2
    tokens = pool_l.shape[1]
    feats = pool_r.shape[1]
    part = lane // 2
    carrier = lax.rem(lane, 2) == 1
    token_at = pl.multiple_of(part * tokens, tokens)
    feat_at = pl.multiple_of(part * feats, feats)
    barrier = pltpu.get_barrier_semaphore()

    for step in range(1, heads):
        pl.semaphore_signal(
            barrier, inc=1, device_id={"head": lax.rem(lane + step, heads)}, device_id_type=MESH
        )
    pl.semaphore_signal(barrier, inc=1, device_id=other, device_id_type=MESH)

    @pl.when(carrier)
    def _():
        def tell(p, carry):
            pl.semaphore_signal(barrier, inc=1, device_id={"req": p}, device_id_type=MESH)
            return carry

        lax.fori_loop(row + 1, rows, tell, 0)

    load_l = pltpu.make_async_copy(
        pool_lat.at[:, pl.ds(token_at, tokens), :], pool_l, pool_sem.at[0]
    )
    load_r = pltpu.make_async_copy(
        pool_rope.at[:, pl.ds(feat_at, feats), :], pool_r, pool_sem.at[1]
    )

    @pl.when(carrier)
    def _():
        load_l.start()
        load_r.start()

    physical = [slot_ref[list_ref[0, j]] for j in range(blocks)]
    column = lax.broadcasted_iota(jnp.int32, own_v.shape, 1)
    own = jnp.zeros(own_v.shape, jnp.int32)
    for j in range(blocks):
        own = jnp.where(column == j, physical[j], own)
    own_v[...] = own

    @pl.when(row > 0)
    def _():
        pl.semaphore_wait(barrier, heads + jnp.where(carrier, row, 0))

    def lat_copy(p, sem_at):
        return pltpu.make_async_remote_copy(
            send_l.at[p], got_l.at[row], lat_send.at[p], lat_recv.at[sem_at], {"req": p}, MESH
        )

    def rope_copy(p, sem_at):
        return pltpu.make_async_remote_copy(
            send_r.at[p], got_r.at[row], rope_send.at[p], rope_recv.at[sem_at], {"req": p}, MESH
        )

    def ask_copy(p):
        return pltpu.make_async_remote_copy(
            own_v, asked_v.at[row], ask_send.at[p], ask_recv.at[row], {"req": p}, MESH
        )

    def chosen(read):
        count = jnp.int32(0)
        first = jnp.int32(0)
        second = jnp.int32(0)
        for j in range(blocks):
            where = read(j)
            here = (where // pool_local) == row
            local = where - row * pool_local
            first = jnp.where(here & (count == 0), local, first)
            second = jnp.where(here & (count == 1), local, second)
            count = count + here.astype(jnp.int32)
        return first, second

    def serve(p, read):
        first, second = chosen(read)
        send_l[p, 0] = pool_l[first]
        send_l[p, 1] = pool_l[second]
        send_r[p] = pool_r[jnp.where(core == 0, first, second)]
        lat_copy(p, row).start()
        rope_copy(p, row).start()

    table_copy = pltpu.make_async_remote_copy(
        table_out, table_in, table_sem.at[0], table_sem.at[1], {"req": lax.rem(row + 1, rows)}, MESH
    )

    @pl.when(carrier)
    def _():
        @pl.when(row > 0)
        def _():
            pl.semaphore_signal(
                hello_sem, inc=1, device_id={"req": row - 1}, device_id_type=MESH
            )

        def ask(p, carry):
            ask_copy(p).start()
            return carry

        lax.fori_loop(0, row, ask, 0)
        load_l.wait()
        load_r.wait()

        @pl.when(row > 0)
        def _():
            table_copy.wait_recv()
            to_s = pltpu.make_async_copy(table_in, table_s, small_sem.at[0])
            to_s.start()
            to_s.wait()

            def below(p, carry):
                serve(p, lambda j: table_s[p, j])
                return carry

            lax.fori_loop(0, row, below, 0)

        @pl.when(row < rows - 1)
        def _():
            line = lax.broadcasted_iota(jnp.int32, table_out.shape, 0)
            mine = jnp.broadcast_to(own_v[0:1, :], table_out.shape)
            known = jnp.where(line < row, table_in[...], 0)
            table_out[...] = jnp.where(line == row, mine, known)
            pl.semaphore_wait(hello_sem, 1)
            table_copy.start()

            def above(p, carry):
                pltpu.make_async_remote_copy(
                    own_v, asked_v.at[p], ask_send.at[p], ask_recv.at[p], {"req": p}, MESH
                ).wait_recv()
                to_s = pltpu.make_async_copy(asked_v.at[p], asked_s, small_sem.at[1])
                to_s.start()
                to_s.wait()
                serve(p, lambda j: asked_s[0, j])
                return carry

            lax.fori_loop(row + 1, rows, above, 0)

        first, second = chosen(lambda j: physical[j])
        got_l[row, 0] = pool_l[first]
        got_l[row, 1] = pool_l[second]
        got_r[row] = pool_r[jnp.where(core == 0, first, second)]

        def arrived(p, carry):
            @pl.when(p != row)
            def _():
                lat_copy(p, p).wait_recv()
                rope_copy(p, p).wait_recv()

            return carry

        lax.fori_loop(0, rows, arrived, 0)

        for j in range(blocks):
            owner = physical[j] // pool_local
            rank = jnp.int32(0)
            for i in range(j):
                rank = rank + (physical[i] // pool_local == owner).astype(jnp.int32)
            lat_mine[j, pl.ds(token_at, tokens), :] = got_l[owner, jnp.minimum(rank, CAP - 1)]
            piece = got_r[owner]
            rope_mine[j, pl.ds(feat_at, feats), :] = jnp.where(
                rank == core, piece, jnp.zeros_like(piece)
            )

    @pl.when(row == 0)
    def _():
        pl.semaphore_wait(barrier, heads)

    new_copies = [
        pltpu.make_async_remote_copy(
            src, dst, snew_send.at[i], snew_recv.at[i], other, MESH
        )
        for i, (src, dst) in enumerate(((new_lat, new_lat_other), (new_rope, new_rope_other)))
    ]
    for copy in new_copies:
        copy.start()

    def lat_piece(k):
        return pl.ds(pl.multiple_of(k * tokens, tokens), tokens)

    def rope_piece(k):
        return pl.ds(pl.multiple_of(k * feats, feats), feats)

    def xlat_copy(k, peer):
        at = lat_piece(k)
        return pltpu.make_async_remote_copy(
            lat_mine.at[:, at, :],
            lat_mine.at[:, at, :],
            xlat_send.at[peer],
            xlat_recv.at[k],
            {"head": peer},
            MESH,
        )

    def xrope_copy(k, peer):
        at = rope_piece(k)
        return pltpu.make_async_remote_copy(
            rope_mine.at[:, at, :],
            rope_mine.at[:, at, :],
            xrope_send.at[peer],
            xrope_recv.at[k],
            {"head": peer},
            MESH,
        )

    def sub_copies(k):
        at, fat = lat_piece(k), rope_piece(k)
        return (
            pltpu.make_async_remote_copy(
                lat_mine.at[:, at, :],
                lat_other.at[:, at, :],
                slat_send.at[k],
                slat_recv.at[k],
                other,
                MESH,
            ),
            pltpu.make_async_remote_copy(
                rope_mine.at[:, fat, :],
                rope_other.at[:, fat, :],
                srope_send.at[k],
                srope_recv.at[k],
                other,
                MESH,
            ),
        )

    order = [0]
    for step in range(heads // 2, 0, -1):
        for peer in (step, heads - step):
            if peer not in order:
                order.append(peer)
    order = order[1:]

    @pl.when(carrier)
    def _():
        for step in order:
            peer = lax.rem(lane + step, heads)
            xlat_copy(part, peer).start()
            xrope_copy(part, peer).start()
        for copy in sub_copies(part):
            copy.start()

    for k in range(carriers):
        mine = carrier & (part == k)

        @pl.when(jnp.logical_not(mine))
        def _(k=k):
            xlat_copy(k, lane).wait_recv()
            xrope_copy(k, lane).wait_recv()
            for copy in sub_copies(k):
                copy.start()

    for k in range(carriers):
        for copy in sub_copies(k):
            copy.wait()
    for copy in new_copies:
        copy.wait()

    @pl.when(carrier)
    def _():
        for step in order:
            peer = lax.rem(lane + step, heads)
            xlat_copy(part, peer).wait_send()
            xrope_copy(part, peer).wait_send()

        def sent(p, carry):
            @pl.when(p != row)
            def _():
                lat_copy(p, row).wait_send()
                rope_copy(p, row).wait_send()

            @pl.when(p < row)
            def _():
                ask_copy(p).wait_send()

            return carry

        lax.fori_loop(0, rows, sent, 0)

        @pl.when(row < rows - 1)
        def _():
            table_copy.wait_send()


def attend(
    scale,
    length_ref,
    q_nope,
    q_rope,
    lat_mine,
    lat_other,
    rope_mine,
    rope_other,
    new_lat,
    new_lat_other,
    new_rope,
    new_rope_other,
    w_uk,
    w_uv,
    out,
    keys,
    rope_even,
    rope_odd,
    bias,
):
    core = lax.axis_index("sub")
    blocks, block, half = lat_mine.shape
    prefix = blocks * block
    queries = q_nope.shape[0]
    total = keys.shape[0]
    here = pl.ds(pl.multiple_of(core * half, half), half)
    there = pl.ds(pl.multiple_of((1 - core) * half, half), half)
    for j in range(blocks):
        keys[pl.ds(j * block, block), here] = lat_mine[j]
        keys[pl.ds(j * block, block), there] = lat_other[j]
    keys[pl.ds(prefix, queries), :] = new_lat[...]
    keys[pl.ds(prefix + queries, queries), :] = new_lat_other[...]

    def put_rope(at, piece):
        turned = piece.astype(F32).T.astype(BF)
        blank = jnp.zeros_like(turned)
        rope_even[pl.ds(at, turned.shape[0]), :] = jnp.concatenate([turned, blank], axis=1)
        rope_odd[pl.ds(at, turned.shape[0]), :] = jnp.concatenate([blank, turned], axis=1)

    for j in range(blocks):
        put_rope(j * block, rope_mine[j] + rope_other[j])
    put_rope(prefix, new_rope[...])
    put_rope(prefix + queries, new_rope_other[...])

    key = lax.broadcasted_iota(jnp.int32, (queries, total), 1)
    query = lax.broadcasted_iota(jnp.int32, (queries, total), 0)
    last = jnp.where(core == 1, total, prefix + queries)
    hidden = F32(-1e30)
    in_prefix = jnp.where(key < length_ref[0], F32(0.0), hidden)
    in_mine = jnp.where(key - prefix <= query, F32(0.0), hidden)
    in_other = jnp.where(key < last, F32(0.0), hidden)
    fresh = jnp.where(key < prefix + queries, in_mine, in_other)
    bias[...] = jnp.where(key < prefix, in_prefix, fresh)

    def pair(i, carry):
        cols = pl.ds(pl.multiple_of(i * 2 * NOPE, 2 * NOPE), 2 * NOPE)
        k2 = jnp.dot(keys[...], w_uk[:, cols], preferred_element_type=F32).astype(BF)
        v2 = jnp.dot(keys[...], w_uv[:, cols], preferred_element_type=F32).astype(BF)
        qr = q_rope[:, pl.ds(pl.multiple_of(i * 2 * ROPE, 2 * ROPE), 2 * ROPE)]
        qn = q_nope[:, cols]
        outs = []
        for e, kr in ((0, rope_even), (1, rope_odd)):
            kcat = jnp.concatenate([k2[:, e * NOPE : (e + 1) * NOPE], kr[...]], axis=1)
            qcat = jnp.concatenate([qn[:, e * NOPE : (e + 1) * NOPE], qr], axis=1)
            s = lax.dot_general(
                qcat, kcat, (((1,), (1,)), ((), ())), preferred_element_type=F32
            )
            s = s * scale + bias[...]
            peak = jnp.max(s, axis=1, keepdims=True)
            expo = jnp.exp(s - peak)
            weights = (expo * (1.0 / jnp.sum(expo, axis=1, keepdims=True))).astype(BF)
            outs.append(
                jnp.dot(
                    weights, v2[:, e * VDIM : (e + 1) * VDIM], preferred_element_type=F32
                ).astype(BF)
            )
        out[:, cols] = jnp.concatenate(outs, axis=1)
        return carry

    lax.fori_loop(0, q_nope.shape[1] // (2 * NOPE), pair, 0)


def shards(
    q_nope,
    q_rope,
    new_latent,
    new_rope,
    pool_latent,
    pool_rope,
    w_uk,
    w_uv,
    block_list,
    prefix_len,
    block_slot,
):
    rows = lax.axis_size("req")
    heads = lax.axis_size("head")
    pool_local, block, half = pool_latent.shape
    blocks = block_list.shape[1]
    queries = q_nope.shape[0]
    carriers = heads // 2
    tokens = block // carriers
    feats = ROPE // carriers
    pool_rope = jnp.swapaxes(pool_rope, 1, 2)
    new_rope = new_rope.T
    vmem = pl.BlockSpec(memory_space=pltpu.VMEM)
    smem = pl.BlockSpec(memory_space=pltpu.SMEM)
    hbm = pl.BlockSpec(memory_space=pl.ANY)
    dma = pltpu.SemaphoreType.DMA
    shape = jax.ShapeDtypeStruct
    lat_mine, lat_other, rope_mine, rope_other, new_lat_other, new_rope_other = pl.pallas_call(
        functools.partial(exchange, blocks, pool_local),
        out_shape=(
            shape((blocks, block, half), BF),
            shape((blocks, block, half), BF),
            shape((blocks, ROPE, block), BF),
            shape((blocks, ROPE, block), BF),
            shape(new_latent.shape, BF),
            shape(new_rope.shape, BF),
        ),
        in_specs=[smem, smem, hbm, hbm, vmem, vmem],
        out_specs=(vmem,) * 6,
        scratch_shapes=[
            pltpu.VMEM((pool_local, tokens, half), BF),
            pltpu.VMEM((pool_local, feats, block), BF),
            pltpu.VMEM((rows, CAP, tokens, half), BF),
            pltpu.VMEM((rows, feats, block), BF),
            pltpu.VMEM((rows, CAP, tokens, half), BF),
            pltpu.VMEM((rows, feats, block), BF),
            pltpu.VMEM((8, 128), jnp.int32),
            pltpu.VMEM((rows, 128), jnp.int32),
            pltpu.VMEM((rows, 128), jnp.int32),
            pltpu.VMEM((rows, 8, 128), jnp.int32),
            pltpu.SMEM((rows, 128), jnp.int32),
            pltpu.SMEM((8, 128), jnp.int32),
            dma((2,)),
            dma((2,)),
            pltpu.SemaphoreType.REGULAR,
            dma((2,)),
            dma((rows,)),
            dma((rows,)),
            dma((rows,)),
            dma((rows,)),
            dma((rows,)),
            dma((rows,)),
            dma((heads,)),
            dma((carriers,)),
            dma((heads,)),
            dma((carriers,)),
            dma((carriers,)),
            dma((carriers,)),
            dma((carriers,)),
            dma((carriers,)),
            dma((2,)),
            dma((2,)),
        ],
        compiler_params=pltpu.CompilerParams(
            collective_id=0, has_side_effects=True, vmem_limit_bytes=16 << 20
        ),
        name="exchange",
    )(block_list, block_slot, pool_latent, pool_rope, new_latent, new_rope)
    total = (blocks * block) + 2 * queries
    return pl.pallas_call(
        functools.partial(attend, 1.0 / math.sqrt(NOPE + ROPE)),
        out_shape=shape(q_nope.shape, BF),
        in_specs=[smem] + [vmem] * 12,
        out_specs=vmem,
        scratch_shapes=[
            pltpu.VMEM((total, 2 * half), BF),
            pltpu.VMEM((total, 2 * ROPE), BF),
            pltpu.VMEM((total, 2 * ROPE), BF),
            pltpu.VMEM((queries, total), F32),
        ],
        compiler_params=pltpu.CompilerParams(vmem_limit_bytes=32 << 20),
        name="attend",
    )(
        prefix_len,
        q_nope,
        q_rope,
        lat_mine,
        lat_other,
        rope_mine,
        rope_other,
        new_latent,
        new_lat_other,
        new_rope,
        new_rope_other,
        w_uk,
        w_uv,
    )


def solution(mesh):
    placed = (
        P(("groups", "req", "sub"), "head"),
        P(("groups", "req", "sub"), "head"),
        P(("groups", "req", "sub"), None),
        P(("groups", "req", "sub"), None),
        P(("groups", "req"), None, "sub"),
        P(("groups", "req"), None, None),
        P(None, "head"),
        P(None, "head"),
        P(("groups", "req"), None),
        P(("groups", "req")),
        P("groups"),
    )
    return jax.shard_map(
        shards,
        mesh=mesh,
        in_specs=placed,
        out_specs=P(("groups", "req", "sub"), "head"),
        check_vma=False,
    )
```

time: 132 us -> 126 us (0.955)
  Pallas kernels: 0 us -> 118 us
  starting transfers between devices: 55.3 us -> 0 us
  waiting for transfers between devices: 29.6 us -> 0 us
  blocking collectives: 17.5 us -> 0 us
  matrix products: 16.2 us -> 0 us
  other arithmetic: 4.02 us -> 0 us
  local copies, waits for them, and re-layouts: 8.51 us -> 6.6 us
    pallas_call x0 -> x2, Pallas kernels: none -> 118 us  [the longest x1 110 us: shards(): pl.pallas_call(functools.partial(exchange, blocks, pool_local), out_shape...]
    all_to_all x3 -> x0, starting transfers between devices: 55.3 us -> none  [the longest x1 44.2 us: shards(): lax.all_to_all(request, 'req', split_axis=0, concat_axis=0, tiled=True)]
    all_to_all x3 -> x0, waiting for transfers between devices: 29.6 us -> none  [the longest x1 17.7 us: side_by_side(): lax.all_to_all(both, axis, split_axis=split_dim, concat_axis=concat_dim,...]
    all_gather x2 -> x0, blocking collectives: 17.5 us -> none  [the longest x1 9.4 us: shards(): prefix_lat = lax.all_gather(prefix_lat, 'sub', axis=2, tiled=True)]
    dot_general x4 -> x0, matrix products: 10.3 us -> none  [the longest x1 3.54 us: shards(): jnp.einsum('hqk,khd->qhd', weights, values, preferred_element_type=jnp.fl...]
    unnamed x16 -> x22, local copies, waits for them, and re-layouts: 0.27 us -> 6.6 us
    sub x1 -> x0, matrix products: 5.9 us -> none  [shards(): expo = jnp.where(visible[None], jnp.exp(scores - peak), jnp.float32(0.0))]
    gather x4 -> x0, local copies, waits for them, and re-layouts: 2.33 us -> none  [the longest x1 0.65 us: shards(): jnp.take(rope_part, asked, axis=0).reshape(owners, CAP, width, -1)]
  transfers between devices with their start and end apart: 3 -> 0, of which waited for: 3 -> 0; matrix products, arithmetic and copies ran while one was open for 3% -> 0% of each run, Pallas kernels for 0% -> 0%
where the time goes in v1:
time: 126 us; the launch traced here: 125 us
  Pallas kernels  118 us (94%)
  local copies, waits for them, and re-layouts  6.6 us (5%)
    pallas_call x1, Pallas kernels, shards(): pl.pallas_call(functools.partial(exchange, blocks, pool_local), out_shape...  110 us
    pallas_call x1, Pallas kernels, shards(): pl.pallas_call(functools.partial(attend, 1.0 / math.sqrt(NOPE + ROPE)), o...  8.14 us
    unnamed x22, local copies, waits for them, and re-layouts  6.6 us

profile of v1, /device:TPU:65, one launch (start us, length us, event | category | flops | bytes accessed | tf_op | source)
XLA Modules:
  0.0 125.2 jit_solution(15604792970457783263)
XLA Ops:
  0.7 0.0 copy-start.9
  0.7 0.0 copy-start.10
  0.7 0.7 copy-done.9
  1.3 0.0 copy-done.10
  1.3 0.0 copy-start
  1.3 1.2 copy-done
  2.6 0.0 copy-start.3
  2.6 0.9 copy-done.3
  3.5 0.0 copy-start.6
  3.5 0.9 copy-done.6
  4.4 0.0 copy-start.8
  4.4 0.7 copy-done.8
  5.1 0.0 copy-start.1
  5.1 0.0 copy-start.4
  5.1 0.0 copy-start.5
  5.1 109.7 %exchange.1 = (bf16[6,128,256]{2,1,0:T(8,128)(2,1)S(1)}, bf16[6,128,256]{2,1,0:T(8,128)(2,1)S(1)}, bf16[6,64,128]{2,1,0:T(8,128)(2,1)S(1)}, bf16[6,64,128]{2,1,0...) custom-call(s32[1,6]{1,0:T(1,128)S(1)} %copy-done.10, s32[256]{0:T(256)S(1)} %copy-done.9, ...), custom_call_target="tpu_custom_call" | custom-call | tf_op jit(solution)/shard_map/exchange/pallas_call | solution.py:467
  114.9 0.0 copy-done.1
  114.9 0.0 copy-done.4
  114.9 0.0 copy-done.5
  114.9 0.0 copy-start.2
  114.9 1.2 copy-done.2
  116.1 0.0 copy-start.7
  116.1 0.9 copy-done.7
  117.0 8.1 %attend.1 = bf16[128,1024]{1,0:T(8,128)(2,1)} custom-call(s32[1]{0:T(128)S(6)} %copy.12.length_ref, bf16[128,1024]{1,0:T(8,128)(2,1)S(1)} %copy-done.5, bf16[128,512]{1,0:T(8,128)(2,1)S(1)} %copy-done.7, bf16[6,128,256]{2,1,0:T(8,128)(2,1)S(1)} %get-tuple-element.11.lat_mine, bf16[6,128,256]{2,1,0:T(8,128)(2,1)S(1)} %get-tuple-element.12.lat_other, ...), custom_call_target="tpu_custom_call" | custom-call | tf_op jit(solution)/shard_map/attend/pallas_call | solution.py:519
Async XLA Ops:
  0.7 0.7 copy-start.9
  0.7 0.7 copy-start.10
  1.3 1.2 copy-start
  2.6 0.9 copy-start.3
  3.5 0.9 copy-start.6
  4.4 0.7 copy-start.8
  5.1 109.7 %copy-start.1 = (bf16[512,1024]{1,0:T(8,128)(2,1)S(1)}, bf16[512,1024]{1,0:T(8,128)(2,1)}, u32[]{:S(2)}) copy-start(bf16[512,1024]{1,0:T(8,128)(2,1)} %w_uk.1) | copy-start | bytes 3145732
  5.1 109.8 %copy-start.4 = (bf16[128,512]{1,0:T(8,128)(2,1)S(1)}, bf16[128,512]{1,0:T(8,128)(2,1)}, u32[]{:S(2)}) copy-start(bf16[128,512]{1,0:T(8,128)(2,1)} %new_lat.3) | copy-start | bytes 393220
  5.1 109.8 %copy-start.5 = (bf16[128,1024]{1,0:T(8,128)(2,1)S(1)}, bf16[128,1024]{1,0:T(8,128)(2,1)}, u32[]{:S(2)}) copy-start(bf16[128,1024]{1,0:T(8,128)(2,1)} %q_nope.1) | copy-start | bytes 786436
  114.9 1.2 copy-start.2
  116.1 0.9 copy-start.7

commit v2 on v1

v2 whole, which is shorter than its diff:
```python
import functools
import math

import jax
import jax.numpy as jnp
from jax import lax
from jax.experimental import pallas as pl
from jax.experimental.pallas import tpu as pltpu
from jax.sharding import PartitionSpec as P

NOPE = 128
ROPE = 64
VDIM = 128
CAP = 2
MESH = pl.DeviceIdType.MESH
BF = jnp.bfloat16
F32 = jnp.float32


def exchange(
    blocks,
    pool_local,
    scale,
    list_hbm,
    slot_hbm,
    pool_lat,
    pool_rope,
    new_lat,
    new_rope,
    length_ref,
    q_nope,
    q_rope,
    w_uk,
    w_uv,
    out,
    lat_mine,
    lat_other,
    rope_mine,
    rope_other,
    new_lat_other,
    new_rope_other,
    new_lat_v,
    new_rope_v,
    keys,
    rope_even,
    rope_odd,
    bias,
    q_nope_v,
    q_rope_v,
    w_uk_v,
    w_uv_v,
    load_sem,
    pool_l,
    pool_r,
    send_l,
    send_r,
    got_l,
    got_r,
    own_v,
    table_in,
    table_out,
    asked_v,
    table_s,
    asked_s,
    list_ref,
    slot_ref,
    pool_sem,
    small_sem,
    hello_sem,
    table_sem,
    ask_send,
    ask_recv,
    lat_send,
    lat_recv,
    rope_send,
    rope_recv,
    xlat_send,
    xlat_recv,
    xrope_send,
    xrope_recv,
    slat_send,
    slat_recv,
    srope_send,
    srope_recv,
    snew_send,
    snew_recv,
):
    rows = lax.axis_size("req")
    heads = lax.axis_size("head")
    row = lax.axis_index("req")
    lane = lax.axis_index("head")
    core = lax.axis_index("sub")
    other = {"sub": 1 - core}
    carriers = heads
    tokens = pool_l.shape[1]
    feats = pool_r.shape[1]
    part = lane
    turn = jnp.where(lane == 0, 1, 0)
    place = lax.rem(row + rows - turn, rows)

    def at(p):
        return lax.rem(p + turn, rows)

    token_at = pl.multiple_of(part * tokens, tokens)
    feat_at = pl.multiple_of(part * feats, feats)
    barrier = pltpu.get_barrier_semaphore()

    for step in range(1, heads):
        pl.semaphore_signal(
            barrier, inc=1, device_id={"head": lax.rem(lane + step, heads)}, device_id_type=MESH
        )
    pl.semaphore_signal(barrier, inc=1, device_id=other, device_id_type=MESH)

    def tell(p, carry):
        pl.semaphore_signal(barrier, inc=1, device_id={"req": at(p)}, device_id_type=MESH)
        return carry

    lax.fori_loop(place + 1, rows, tell, 0)

    load_l = pltpu.make_async_copy(
        pool_lat.at[:, pl.ds(token_at, tokens), :], pool_l, pool_sem.at[0]
    )
    load_r = pltpu.make_async_copy(
        pool_rope.at[:, pl.ds(feat_at, feats), :], pool_r, pool_sem.at[1]
    )

    load_l.start()
    load_r.start()
    loads = [
        pltpu.make_async_copy(src, dst, load_sem.at[i])
        for i, (src, dst) in enumerate(
            (
                (new_lat, new_lat_v),
                (new_rope, new_rope_v),
                (w_uk, w_uk_v),
                (q_nope, q_nope_v),
                (q_rope, q_rope_v),
                (w_uv, w_uv_v),
            )
        )
    ]
    for load in loads:
        load.start()

    to_list = pltpu.make_async_copy(list_hbm, list_ref, small_sem.at[0])
    to_slot = pltpu.make_async_copy(slot_hbm, slot_ref, small_sem.at[1])
    to_list.start()
    to_slot.start()
    to_list.wait()
    to_slot.wait()
    physical = [slot_ref[list_ref[0, j]] for j in range(blocks)]
    column = lax.broadcasted_iota(jnp.int32, own_v.shape, 1)
    own = jnp.zeros(own_v.shape, jnp.int32)
    for j in range(blocks):
        own = jnp.where(column == j, physical[j], own)
    own_v[...] = own

    @pl.when(place > 0)
    def _():
        pl.semaphore_wait(barrier, heads + place)

    def lat_copy(p, sem_at):
        return pltpu.make_async_remote_copy(
            send_l.at[p], got_l.at[row], lat_send.at[p], lat_recv.at[sem_at], {"req": p}, MESH
        )

    def rope_copy(p, sem_at):
        return pltpu.make_async_remote_copy(
            send_r.at[p], got_r.at[row], rope_send.at[p], rope_recv.at[sem_at], {"req": p}, MESH
        )

    def ask_copy(p):
        return pltpu.make_async_remote_copy(
            own_v, asked_v.at[row], ask_send.at[p], ask_recv.at[row], {"req": p}, MESH
        )

    def chosen(read):
        count = jnp.int32(0)
        first = jnp.int32(0)
        second = jnp.int32(0)
        for j in range(blocks):
            where = read(j)
            local = where - row * pool_local
            here = (local >= 0) & (local < pool_local)
            first = jnp.where(here & (count == 0), local, first)
            second = jnp.where(here & (count == 1), local, second)
            count = count + here.astype(jnp.int32)
        return first, second

    def serve(p, read):
        first, second = chosen(read)
        send_l[p, 0] = pool_l[first]
        send_l[p, 1] = pool_l[second]
        send_r[p] = pool_r[jnp.where(core == 0, first, second)]
        lat_copy(p, row).start()
        rope_copy(p, row).start()

    table_copy = pltpu.make_async_remote_copy(
        table_out, table_in, table_sem.at[0], table_sem.at[1], {"req": lax.rem(row + 1, rows)}, MESH
    )

    @pl.when(place > 0)
    def _():
        pl.semaphore_signal(
            hello_sem, inc=1, device_id={"req": at(place - 1)}, device_id_type=MESH
        )

    def ask(p, carry):
        ask_copy(at(p)).start()
        return carry

    lax.fori_loop(0, place, ask, 0)
    load_l.wait()
    load_r.wait()

    @pl.when(place > 0)
    def _():
        table_copy.wait_recv()

    line = lax.broadcasted_iota(jnp.int32, table_out.shape, 0)
    mine = jnp.broadcast_to(own_v[0:1, :], table_out.shape)
    below_me = lax.rem(line + rows - turn, rows) < place
    known = jnp.where(below_me, table_in[...], 0)
    table_out[...] = jnp.where(line == row, mine, known)

    @pl.when(place < rows - 1)
    def _():
        pl.semaphore_wait(hello_sem, 1)
        table_copy.start()

    @pl.when(place > 0)
    def _():
        to_s = pltpu.make_async_copy(table_in, table_s, small_sem.at[0])
        to_s.start()
        to_s.wait()

        def below(p, carry):
            r = at(p)
            serve(r, lambda j: table_s[r, j])
            return carry

        lax.fori_loop(0, place, below, 0)

    @pl.when(place < rows - 1)
    def _():

        def above(p, carry):
            r = at(p)
            pltpu.make_async_remote_copy(
                own_v, asked_v.at[r], ask_send.at[r], ask_recv.at[r], {"req": r}, MESH
            ).wait_recv()
            to_s = pltpu.make_async_copy(asked_v.at[r], asked_s, small_sem.at[1])
            to_s.start()
            to_s.wait()
            serve(r, lambda j: asked_s[0, j])
            return carry

        lax.fori_loop(place + 1, rows, above, 0)

    first, second = chosen(lambda j: physical[j])
    got_l[row, 0] = pool_l[first]
    got_l[row, 1] = pool_l[second]
    got_r[row] = pool_r[jnp.where(core == 0, first, second)]

    def arrived(p, carry):
        @pl.when(p != row)
        def _():
            lat_copy(p, p).wait_recv()
            rope_copy(p, p).wait_recv()

        return carry

    lax.fori_loop(0, rows, arrived, 0)

    for j in range(blocks):
        owner = physical[j] // pool_local
        rank = jnp.int32(0)
        for i in range(j):
            rank = rank + (physical[i] // pool_local == owner).astype(jnp.int32)
        lat_mine[j, pl.ds(token_at, tokens), :] = got_l[owner, jnp.minimum(rank, CAP - 1)]
        piece = got_r[owner]
        rope_mine[j, pl.ds(feat_at, feats), :] = jnp.where(
            rank == core, piece, jnp.zeros_like(piece)
        )

    @pl.when(place == 0)
    def _():
        pl.semaphore_wait(barrier, heads)

    for load in loads:
        load.wait()
    new_copies = [
        pltpu.make_async_remote_copy(
            src, dst, snew_send.at[i], snew_recv.at[i], other, MESH
        )
        for i, (src, dst) in enumerate(((new_lat_v, new_lat_other), (new_rope_v, new_rope_other)))
    ]
    for copy in new_copies:
        copy.start()

    def lat_piece(k):
        return pl.ds(pl.multiple_of(k * tokens, tokens), tokens)

    def rope_piece(k):
        return pl.ds(pl.multiple_of(k * feats, feats), feats)

    def xlat_copy(k, peer):
        at = lat_piece(k)
        return pltpu.make_async_remote_copy(
            lat_mine.at[:, at, :],
            lat_mine.at[:, at, :],
            xlat_send.at[peer],
            xlat_recv.at[k],
            {"head": peer},
            MESH,
        )

    def xrope_copy(k, peer):
        at = rope_piece(k)
        return pltpu.make_async_remote_copy(
            rope_mine.at[:, at, :],
            rope_mine.at[:, at, :],
            xrope_send.at[peer],
            xrope_recv.at[k],
            {"head": peer},
            MESH,
        )

    def sub_copies(k):
        at, fat = lat_piece(k), rope_piece(k)
        return (
            pltpu.make_async_remote_copy(
                lat_mine.at[:, at, :],
                lat_other.at[:, at, :],
                slat_send.at[k],
                slat_recv.at[k],
                other,
                MESH,
            ),
            pltpu.make_async_remote_copy(
                rope_mine.at[:, fat, :],
                rope_other.at[:, fat, :],
                srope_send.at[k],
                srope_recv.at[k],
                other,
                MESH,
            ),
        )

    order = [0]
    for step in range(heads // 2, 0, -1):
        for peer in (step, heads - step):
            if peer not in order:
                order.append(peer)
    order = order[1:]

    for step in order:
        peer = lax.rem(lane + step, heads)
        xlat_copy(part, peer).start()
        xrope_copy(part, peer).start()
    for copy in sub_copies(part):
        copy.start()

    for k in range(carriers):

        @pl.when(part != k)
        def _(k=k):
            xlat_copy(k, lane).wait_recv()
            xrope_copy(k, lane).wait_recv()
            for copy in sub_copies(k):
                copy.start()

    for k in range(carriers):
        for copy in sub_copies(k):
            copy.wait()
    for copy in new_copies:
        copy.wait()

    blocks, block, half = lat_mine.shape
    prefix = blocks * block
    queries = q_nope.shape[0]
    total = keys.shape[0]
    here = pl.ds(pl.multiple_of(core * half, half), half)
    there = pl.ds(pl.multiple_of((1 - core) * half, half), half)
    for j in range(blocks):
        keys[pl.ds(j * block, block), here] = lat_mine[j]
        keys[pl.ds(j * block, block), there] = lat_other[j]
    keys[pl.ds(prefix, queries), :] = new_lat_v[...]
    keys[pl.ds(prefix + queries, queries), :] = new_lat_other[...]

    def put_rope(at, piece):
        turned = piece.astype(F32).T.astype(BF)
        blank = jnp.zeros_like(turned)
        rope_even[pl.ds(at, turned.shape[0]), :] = jnp.concatenate([turned, blank], axis=1)
        rope_odd[pl.ds(at, turned.shape[0]), :] = jnp.concatenate([blank, turned], axis=1)

    for j in range(blocks):
        put_rope(j * block, rope_mine[j] + rope_other[j])
    put_rope(prefix, new_rope_v[...])
    put_rope(prefix + queries, new_rope_other[...])

    key = lax.broadcasted_iota(jnp.int32, (queries, total), 1)
    query = lax.broadcasted_iota(jnp.int32, (queries, total), 0)
    last = jnp.where(core == 1, total, prefix + queries)
    hidden = F32(-1e30)
    in_prefix = jnp.where(key < length_ref[0], F32(0.0), hidden)
    in_mine = jnp.where(key - prefix <= query, F32(0.0), hidden)
    in_other = jnp.where(key < last, F32(0.0), hidden)
    fresh = jnp.where(key < prefix + queries, in_mine, in_other)
    bias[...] = jnp.where(key < prefix, in_prefix, fresh)

    def pair(i, carry):
        cols = pl.ds(pl.multiple_of(i * 2 * NOPE, 2 * NOPE), 2 * NOPE)
        k2 = jnp.dot(keys[...], w_uk_v[:, cols], preferred_element_type=F32).astype(BF)
        v2 = jnp.dot(keys[...], w_uv_v[:, cols], preferred_element_type=F32).astype(BF)
        qr = q_rope_v[:, pl.ds(pl.multiple_of(i * 2 * ROPE, 2 * ROPE), 2 * ROPE)]
        qn = q_nope_v[:, cols]
        outs = []
        for e, kr in ((0, rope_even), (1, rope_odd)):
            kcat = jnp.concatenate([k2[:, e * NOPE : (e + 1) * NOPE], kr[...]], axis=1)
            qcat = jnp.concatenate([qn[:, e * NOPE : (e + 1) * NOPE], qr], axis=1)
            s = lax.dot_general(
                qcat, kcat, (((1,), (1,)), ((), ())), preferred_element_type=F32
            )
            s = s * scale + bias[...]
            peak = jnp.max(s, axis=1, keepdims=True)
            expo = jnp.exp(s - peak)
            weights = (expo * (1.0 / jnp.sum(expo, axis=1, keepdims=True))).astype(BF)
            outs.append(
                jnp.dot(
                    weights, v2[:, e * VDIM : (e + 1) * VDIM], preferred_element_type=F32
                ).astype(BF)
            )
        out[:, cols] = jnp.concatenate(outs, axis=1)
        return carry

    lax.fori_loop(0, q_nope.shape[1] // (2 * NOPE), pair, 0)

    for step in order:
        peer = lax.rem(lane + step, heads)
        xlat_copy(part, peer).wait_send()
        xrope_copy(part, peer).wait_send()

    def sent(p, carry):
        r = at(p)

        @pl.when(p != place)
        def _():
            lat_copy(r, row).wait_send()
            rope_copy(r, row).wait_send()

        @pl.when(p < place)
        def _():
            ask_copy(r).wait_send()

        return carry

    lax.fori_loop(0, rows, sent, 0)

    @pl.when(place < rows - 1)
    def _():
        table_copy.wait_send()


def shards(
    q_nope,
    q_rope,
    new_latent,
    new_rope,
    pool_latent,
    pool_rope,
    w_uk,
    w_uv,
    block_list,
    prefix_len,
    block_slot,
):
    rows = lax.axis_size("req")
    heads = lax.axis_size("head")
    pool_local, block, half = pool_latent.shape
    blocks = block_list.shape[1]
    queries = q_nope.shape[0]
    carriers = heads
    tokens = block // carriers
    feats = ROPE // carriers
    pool_rope = jnp.swapaxes(pool_rope, 1, 2)
    new_rope = new_rope.T
    vmem = pl.BlockSpec(memory_space=pltpu.VMEM)
    smem = pl.BlockSpec(memory_space=pltpu.SMEM)
    hbm = pl.BlockSpec(memory_space=pltpu.HBM)
    dma = pltpu.SemaphoreType.DMA
    shape = jax.ShapeDtypeStruct
    total = (blocks * block) + 2 * queries
    return pl.pallas_call(
        functools.partial(exchange, blocks, pool_local, 1.0 / math.sqrt(NOPE + ROPE)),
        out_shape=shape(q_nope.shape, BF),
        in_specs=[hbm] * 6 + [smem] + [hbm] * 4,
        out_specs=vmem,
        scratch_shapes=[
            pltpu.VMEM((blocks, block, half), BF),
            pltpu.VMEM((blocks, block, half), BF),
            pltpu.VMEM((blocks, ROPE, block), BF),
            pltpu.VMEM((blocks, ROPE, block), BF),
            pltpu.VMEM(new_latent.shape, BF),
            pltpu.VMEM(new_rope.shape, BF),
            pltpu.VMEM(new_latent.shape, BF),
            pltpu.VMEM(new_rope.shape, BF),
            pltpu.VMEM((total, 2 * half), BF),
            pltpu.VMEM((total, 2 * ROPE), BF),
            pltpu.VMEM((total, 2 * ROPE), BF),
            pltpu.VMEM((queries, total), F32),
            pltpu.VMEM(q_nope.shape, BF),
            pltpu.VMEM(q_rope.shape, BF),
            pltpu.VMEM(w_uk.shape, BF),
            pltpu.VMEM(w_uv.shape, BF),
            dma((6,)),
            pltpu.VMEM((pool_local, tokens, half), BF),
            pltpu.VMEM((pool_local, feats, block), BF),
            pltpu.VMEM((rows, CAP, tokens, half), BF),
            pltpu.VMEM((rows, feats, block), BF),
            pltpu.VMEM((rows, CAP, tokens, half), BF),
            pltpu.VMEM((rows, feats, block), BF),
            pltpu.VMEM((8, 128), jnp.int32),
            pltpu.VMEM((rows, 128), jnp.int32),
            pltpu.VMEM((rows, 128), jnp.int32),
            pltpu.VMEM((rows, 8, 128), jnp.int32),
            pltpu.SMEM((rows, 128), jnp.int32),
            pltpu.SMEM((8, 128), jnp.int32),
            pltpu.SMEM(block_list.shape, jnp.int32),
            pltpu.SMEM(block_slot.shape, jnp.int32),
            dma((2,)),
            dma((2,)),
            pltpu.SemaphoreType.REGULAR,
            dma((2,)),
            dma((rows,)),
            dma((rows,)),
            dma((rows,)),
            dma((rows,)),
            dma((rows,)),
            dma((rows,)),
            dma((heads,)),
            dma((carriers,)),
            dma((heads,)),
            dma((carriers,)),
            dma((carriers,)),
            dma((carriers,)),
            dma((carriers,)),
            dma((carriers,)),
            dma((2,)),
            dma((2,)),
        ],
        compiler_params=pltpu.CompilerParams(
            collective_id=0, has_side_effects=True, vmem_limit_bytes=62 << 20
        ),
        name="fused",
    )(
        block_list,
        block_slot,
        pool_latent,
        pool_rope,
        new_latent,
        new_rope,
        prefix_len,
        q_nope,
        q_rope,
        w_uk,
        w_uv,
    )


def solution(mesh):
    placed = (
        P(("groups", "req", "sub"), "head"),
        P(("groups", "req", "sub"), "head"),
        P(("groups", "req", "sub"), None),
        P(("groups", "req", "sub"), None),
        P(("groups", "req"), None, "sub"),
        P(("groups", "req"), None, None),
        P(None, "head"),
        P(None, "head"),
        P(("groups", "req"), None),
        P(("groups", "req")),
        P("groups"),
    )
    return jax.shard_map(
        shards,
        mesh=mesh,
        in_specs=placed,
        out_specs=P(("groups", "req", "sub"), "head"),
        check_vma=False,
    )
```

time: 126 us -> 86.2 us (0.68)
  the two profiles are of different devices: /device:TPU:65 before, /device:TPU:67 now
where the time goes in v2:
time: 86.2 us; the launch traced here: 86.1 us
  Pallas kernels  83.7 us (97%)
  local copies, waits for them, and re-layouts  1.67 us (2%)
    pallas_call x1, Pallas kernels, shards(): pl.pallas_call(functools.partial(exchange, blocks, pool_local, 1.0 / math...  83.7 us

profile of v2, /device:TPU:67, one launch (start us, length us, event | category | flops | bytes accessed | tf_op | source)
XLA Modules:
  0.0 86.1 jit_solution(14787175555739311964)
XLA Ops:
  0.7 83.7 %fused.1 = bf16[128,1024]{1,0:T(8,128)(2,1)} custom-call(s32[1,6]{1,0:T(1,128)} %list_hbm.1, s32[256]{0:T(256)} %slot_hbm.1, bf16[16,128,256]{2,1,0:T(8,128)(2,1)} %pool_lat.1, bf16[16,64,128]{2,1,0:T(8,128)(2,1)} %bitcast.2, bf16[128,512]{1,0:T(8,128)(2,1)} %new_lat.1, bf16[64,128]{1,0:T(8,128)(2,1)} %bitcast.3, s32[1]{0:T(128)S(6)} %copy.13.length_ref, ...), custom_call_target="tpu_custom_call" | custom-call | tf_op jit(solution)/shard_map/fused/pallas_call | solution.py:494
  84.4 1.7 %copy.14 = bf16[128,1024]{1,0:T(8,128)(2,1)} copy(bf16[128,1024]{1,0:T(8,128)(2,1)} %fused.1) | data formatting | bytes 524288

commit v3 on v2

--- a/solution.py
+++ b/solution.py
@@ -12,6 +12,7 @@
 ROPE = 64
 VDIM = 128
 CAP = 2
+EARLY = 4
 MESH = pl.DeviceIdType.MESH
 BF = jnp.bfloat16
 F32 = jnp.float32
@@ -57,6 +58,7 @@
     got_l,
     got_r,
     own_v,
+    near_v,
     table_in,
     table_out,
     asked_v,
@@ -67,6 +69,7 @@
     pool_sem,
     small_sem,
     hello_sem,
+    near_sem,
     table_sem,
     ask_send,
     ask_recv,
@@ -95,7 +98,7 @@
     tokens = pool_l.shape[1]
     feats = pool_r.shape[1]
     part = lane
-    turn = jnp.where(lane == 0, 1, 0)
+    turn = jnp.where((lane == 0) & (core == 0), 1, 0)
     place = lax.rem(row + rows - turn, rows)
 
     def at(p):
@@ -196,14 +199,27 @@
         rope_copy(p, row).start()
 
     table_copy = pltpu.make_async_remote_copy(
-        table_out, table_in, table_sem.at[0], table_sem.at[1], {"req": lax.rem(row + 1, rows)}, MESH
+        table_out,
+        table_in,
+        table_sem.at[0],
+        table_sem.at[1],
+        {"req": at(lax.rem(place + 2, rows))},
+        MESH,
     )
-
-    @pl.when(place > 0)
-    def _():
-        pl.semaphore_signal(
-            hello_sem, inc=1, device_id={"req": at(place - 1)}, device_id_type=MESH
-        )
+    near_copy = pltpu.make_async_remote_copy(
+        own_v, near_v, near_sem.at[0], near_sem.at[1], {"req": at(lax.rem(place + 1, rows))}, MESH
+    )
+
+    for step in (1, 2):
+
+        @pl.when(place >= step)
+        def _(step=step):
+            pl.semaphore_signal(
+                hello_sem.at[step - 1],
+                inc=1,
+                device_id={"req": at(place - step)},
+                device_id_type=MESH,
+            )
 
     def ask(p, carry):
         ask_copy(at(p)).start()
@@ -213,33 +229,47 @@
     load_l.wait()
     load_r.wait()
 
+    @pl.when(place < rows - 1)
+    def _():
+        pl.semaphore_wait(hello_sem.at[0], 1)
+        near_copy.start()
+
+    @pl.when(place > 1)
+    def _():
+        table_copy.wait_recv()
+
     @pl.when(place > 0)
     def _():
-        table_copy.wait_recv()
+        near_copy.wait_recv()
 
     line = lax.broadcasted_iota(jnp.int32, table_out.shape, 0)
+    line_place = lax.rem(line + rows - turn, rows)
     mine = jnp.broadcast_to(own_v[0:1, :], table_out.shape)
-    below_me = lax.rem(line + rows - turn, rows) < place
-    known = jnp.where(below_me, table_in[...], 0)
+    near = jnp.broadcast_to(near_v[0:1, :], table_out.shape)
+    known = jnp.where(line_place < place - 1, table_in[...], 0)
+    known = jnp.where(line_place == place - 1, near, known)
     table_out[...] = jnp.where(line == row, mine, known)
 
-    @pl.when(place < rows - 1)
-    def _():
-        pl.semaphore_wait(hello_sem, 1)
-        table_copy.start()
+    def below(p, carry):
+        r = at(p)
+        serve(r, lambda j: table_s[r, j])
+        return carry
+
+    early = jnp.minimum(place, EARLY)
 
     @pl.when(place > 0)
     def _():
-        to_s = pltpu.make_async_copy(table_in, table_s, small_sem.at[0])
+        to_s = pltpu.make_async_copy(table_out, table_s, small_sem.at[0])
         to_s.start()
         to_s.wait()
-
-        def below(p, carry):
-            r = at(p)
-            serve(r, lambda j: table_s[r, j])
-            return carry
-
-        lax.fori_loop(0, place, below, 0)
+        lax.fori_loop(0, early, below, 0)
+
+    @pl.when(place < rows - 2)
+    def _():
+        pl.semaphore_wait(hello_sem.at[1], 1)
+        table_copy.start()
+
+    lax.fori_loop(early, place, below, 0)
 
     @pl.when(place < rows - 1)
     def _():
@@ -458,6 +488,10 @@
     lax.fori_loop(0, rows, sent, 0)
 
     @pl.when(place < rows - 1)
+    def _():
+        near_copy.wait_send()
+
+    @pl.when(place < rows - 2)
     def _():
         table_copy.wait_send()
 
@@ -521,6 +555,7 @@
             pltpu.VMEM((rows, CAP, tokens, half), BF),
             pltpu.VMEM((rows, feats, block), BF),
             pltpu.VMEM((8, 128), jnp.int32),
+            pltpu.VMEM((8, 128), jnp.int32),
             pltpu.VMEM((rows, 128), jnp.int32),
             pltpu.VMEM((rows, 128), jnp.int32),
             pltpu.VMEM((rows, 8, 128), jnp.int32),
@@ -530,7 +565,8 @@
             pltpu.SMEM(block_slot.shape, jnp.int32),
             dma((2,)),
             dma((2,)),
-            pltpu.SemaphoreType.REGULAR,
+            pltpu.SemaphoreType.REGULAR((2,)),
+            dma((2,)),
             dma((2,)),
             dma((rows,)),
             dma((rows,)),

time: 86.2 us -> 83.5 us (0.969)
  the two profiles are of different devices: /device:TPU:67 before, /device:TPU:65 now
where the time goes in v3:
time: 83.5 us; the launch traced here: 83.3 us
  Pallas kernels  80.9 us (97%)
  local copies, waits for them, and re-layouts  1.67 us (2%)
    pallas_call x1, Pallas kernels, shards(): pl.pallas_call(functools.partial(exchange, blocks, pool_local, 1.0 / math...  80.9 us
    unnamed x1, local copies, waits for them, and re-layouts  1.67 us

profile of v3, /device:TPU:65, one launch (start us, length us, event | category | flops | bytes accessed | tf_op | source)
XLA Modules:
  0.0 83.3 jit_solution(5803437578142526020)
XLA Ops:
  0.7 80.9 %fused.1 = bf16[128,1024]{1,0:T(8,128)(2,1)} custom-call(s32[1,6]{1,0:T(1,128)} %list_hbm.1, s32[256]{0:T(256)} %slot_hbm.1, bf16[16,128,256]{2,1,0:T(8,128)(2,1)} %pool_lat.1, bf16[16,64,128]{2,1,0:T(8,128)(2,1)} %bitcast.2, bf16[128,512]{1,0:T(8,128)(2,1)} %new_lat.1, bf16[64,128]{1,0:T(8,128)(2,1)} %bitcast.3, s32[1]{0:T(128)S(6)} %copy.13.length_ref, ...), custom_call_target="tpu_custom_call" | custom-call | tf_op jit(solution)/shard_map/fused/pallas_call | solution.py:528
  81.6 1.7 %copy.14 = bf16[128,1024]{1,0:T(8,128)(2,1)} copy(bf16[128,1024]{1,0:T(8,128)(2,1)} %fused.1) | data formatting | bytes 524288

commit v4 on v3

--- a/solution.py
+++ b/solution.py
@@ -271,6 +271,18 @@
 
     lax.fori_loop(early, place, below, 0)
 
+    fresh_rows = q_nope.shape[0]
+    ahead_rows = blocks * lat_mine.shape[1]
+    key = lax.broadcasted_iota(jnp.int32, (fresh_rows, keys.shape[0]), 1)
+    query = lax.broadcasted_iota(jnp.int32, (fresh_rows, keys.shape[0]), 0)
+    last = jnp.where(core == 1, keys.shape[0], ahead_rows + fresh_rows)
+    hidden = F32(-1e30)
+    in_prefix = jnp.where(key < length_ref[0], F32(0.0), hidden)
+    in_mine = jnp.where(key - ahead_rows <= query, F32(0.0), hidden)
+    in_other = jnp.where(key < last, F32(0.0), hidden)
+    fresh = jnp.where(key < ahead_rows + fresh_rows, in_mine, in_other)
+    bias[...] = jnp.where(key < ahead_rows, in_prefix, fresh)
+
     @pl.when(place < rows - 1)
     def _():
 
@@ -428,16 +440,6 @@
         put_rope(j * block, rope_mine[j] + rope_other[j])
     put_rope(prefix, new_rope_v[...])
     put_rope(prefix + queries, new_rope_other[...])
-
-    key = lax.broadcasted_iota(jnp.int32, (queries, total), 1)
-    query = lax.broadcasted_iota(jnp.int32, (queries, total), 0)
-    last = jnp.where(core == 1, total, prefix + queries)
-    hidden = F32(-1e30)
-    in_prefix = jnp.where(key < length_ref[0], F32(0.0), hidden)
-    in_mine = jnp.where(key - prefix <= query, F32(0.0), hidden)
-    in_other = jnp.where(key < last, F32(0.0), hidden)
-    fresh = jnp.where(key < prefix + queries, in_mine, in_other)
-    bias[...] = jnp.where(key < prefix, in_prefix, fresh)
 
     def pair(i, carry):
         cols = pl.ds(pl.multiple_of(i * 2 * NOPE, 2 * NOPE), 2 * NOPE)
@@ -464,7 +466,7 @@
         out[:, cols] = jnp.concatenate(outs, axis=1)
         return carry
 
-    lax.fori_loop(0, q_nope.shape[1] // (2 * NOPE), pair, 0)
+    lax.fori_loop(0, q_nope.shape[1] // (2 * NOPE), pair, 0, unroll=True)
 
     for step in order:
         peer = lax.rem(lane + step, heads)

time: 83.5 us -> 82.8 us (level)
  no operation moved by 1% of the time
where the time goes in v4:
time: 82.8 us; the launch traced here: 82.5 us
  Pallas kernels  80.2 us (97%)
  local copies, waits for them, and re-layouts  1.67 us (2%)
    pallas_call x1, Pallas kernels, shards(): pl.pallas_call(functools.partial(exchange, blocks, pool_local, 1.0 / math...  80.2 us
    unnamed x1, local copies, waits for them, and re-layouts  1.67 us

profile of v4, /device:TPU:65, one launch (start us, length us, event | category | flops | bytes accessed | tf_op | source)
XLA Modules:
  0.0 82.5 jit_solution(5147928347499093444)
XLA Ops:
  0.7 80.2 %fused.1 = bf16[128,1024]{1,0:T(8,128)(2,1)} custom-call(s32[1,6]{1,0:T(1,128)} %list_hbm.1, s32[256]{0:T(256)} %slot_hbm.1, bf16[16,128,256]{2,1,0:T(8,128)(2,1)} %pool_lat.1, bf16[16,64,128]{2,1,0:T(8,128)(2,1)} %bitcast.2, bf16[128,512]{1,0:T(8,128)(2,1)} %new_lat.1, bf16[64,128]{1,0:T(8,128)(2,1)} %bitcast.3, s32[1]{0:T(128)S(6)} %copy.13.length_ref, ...), custom_call_target="tpu_custom_call" | custom-call | tf_op jit(solution)/shard_map/fused/pallas_call | solution.py:530
  80.9 1.7 %copy.14 = bf16[128,1024]{1,0:T(8,128)(2,1)} copy(bf16[128,1024]{1,0:T(8,128)(2,1)} %fused.1) | data formatting | bytes 524288
